TPU v7x, 32 devices: a whole 2x2x4 slice. The times are simulated.
32 devices in a mesh: row: 4 (over y, core), col: 8 (over z, x).
Axes of the slice: x: 2, y: 2, z: 4, core: 2. Of those that a mesh axis runs over, the one named last changes fastest.
Arguments:
- matrix: float32 [16384, 16384], P('row', 'col'), as said below
Outputs:
- hess_panel: float32 [16384, 8], P('row')
- reflectors: float32 [16384, 8], P('row')
- wy_products: float32 [16384, 8], P('row')
- wy_factor: float32 [8, 8], replicated
Inputs may be any that keep to these rules, and one draw needn't show every extreme that they name: Entries matrix[i+1, i] lie within 2.5 +- 6 / sqrt(16384); every other entry within +- 6 / sqrt(16384).
All inputs are finite; a program needn't handle non-finite values.
Results may differ from a plain program's by a relative error of at most 0.0003.
Values sent between devices are 32-bit elements; how exact they have to be, the bound alone decides.
A program may use at most 128 MiB of HBM per device.

v0:
```python
import jax
import jax.numpy as jnp
from jax import lax
from jax.sharding import PartitionSpec as P

NB = 8


def spread(value, axis, root):
    mine = lax.axis_index(axis) == root
    return lax.psum(jnp.where(mine, value, jnp.zeros_like(value)), axis)


def shards(matrix):
    exact = lax.Precision.HIGHEST
    rows_local, cols_local = matrix.shape
    row_ids = lax.axis_index("row") * rows_local + lax.iota(jnp.int32, rows_local)
    panel = spread(matrix[:, :NB], "col", 0)
    top_ids = lax.iota(jnp.int32, NB + 1)
    picker = (row_ids[None, :] == top_ids[:, None]).astype(jnp.float32)
    refl = jnp.zeros((rows_local, NB), jnp.float32)
    wy_prod = jnp.zeros((rows_local, NB), jnp.float32)
    factor = jnp.zeros((NB, NB), jnp.float32)
    refl_top = jnp.zeros((NB + 1, NB), jnp.float32)
    gram = jnp.zeros((NB, NB), jnp.float32)
    columns = []
    for column in range(NB):
        current = panel[:, column] - jnp.dot(wy_prod, refl_top[column], precision=exact)
        if column > 0:
            inner = lax.psum(jnp.dot(current, refl, precision=exact), "row")
            current = current - jnp.dot(
                refl, jnp.dot(inner, factor, precision=exact), precision=exact
            )
        below = jnp.where(row_ids > column, current, jnp.float32(0.0))
        sumsq, leading = lax.psum(
            (
                jnp.sum(below * below),
                jnp.sum(jnp.where(row_ids == column + 1, current, jnp.float32(0.0))),
            ),
            "row",
        )
        masked = jnp.where(row_ids > column, current, jnp.float32(0.0))
        length = jnp.sqrt(sumsq)
        orient = jnp.where(leading >= 0, jnp.float32(1.0), jnp.float32(-1.0))
        pivot_value = -orient * length
        vector = masked + jnp.where(row_ids == column + 1, orient * length, jnp.float32(0.0))
        vector = vector / jnp.sqrt(length * (length + jnp.abs(leading)))
        start = lax.axis_index("col") * cols_local
        received = spread(vector, "row", start // rows_local)
        piece = lax.dynamic_slice_in_dim(received, start % rows_local, cols_local, 0)
        coupling, vec_top = lax.psum(
            (jnp.dot(vector, refl, precision=exact), jnp.dot(picker, vector, precision=exact)),
            "row",
        )
        image = lax.psum(jnp.dot(matrix, piece, precision=exact), "col")
        new_y = image - jnp.dot(wy_prod, coupling, precision=exact)
        new_t = -jnp.dot(factor, coupling, precision=exact)
        factor = factor.at[:, column].set(new_t).at[column, column].set(jnp.float32(1.0))
        gram = (
            gram.at[:, column]
            .set(coupling)
            .at[column, :]
            .set(coupling)
            .at[column, column]
            .set(jnp.float32(2.0))
        )
        wy_prod = wy_prod.at[:, column].set(new_y)
        refl = refl.at[:, column].set(vector)
        refl_top = refl_top.at[:, column].set(vec_top)
        columns.append(
            jnp.where(
                row_ids <= column,
                current,
                jnp.where(row_ids == column + 1, pivot_value, jnp.float32(0.0)),
            )
        )
    return (jnp.stack(columns, axis=1), refl, wy_prod, factor)


def solution(mesh):
    return jax.shard_map(
        shards,
        mesh=mesh,
        in_specs=(P("row", "col"),),
        out_specs=(P("row", None), P("row", None), P("row", None), P()),
        check_vma=False,
    )
```

profile of v0, /device:TPU:0, one launch (start us, length us, event | category | flops | bytes accessed | tf_op | source)
XLA Modules:
  0.0 897.8 jit_solution(13445658246605330233)
XLA Ops:
  15.5 101.1 %all-reduce.22.cloned.1.call-done = f32[4096,8]{1,0:T(8,128)} async-done(((f32[4096,8]{1,0:T(8,128)}), f32[4096,8]{1,0:T(8,128)}) %all-reduce.22.cloned.1.call-update) | async-done | bytes 131088 | tf_op jit(solution)/shard_map/psum | solution.py:11
  116.7 15.4 %slice_reduce_fusion = (f32[4096]{0:T(1024)S(1)}, f32[4096]{0:T(1024)S(1)}, f32[4096]{0:T(1024)S(1)}, f32[4096]{0:T(1024)S(1)}, f32[4096]{0:T(1024)S(1)}, /*inde...) fusion(f32[4096,8]{1,0:T(8,128)} %all-reduce.22.cloned.1.call-done), kind=kLoop, calls=%fused_computation | loop fusion | bytes 262144 | tf_op jit(solution)/shard_map/slice | solution.py:28
  133.3 6.8 all-reduce.19
  143.5 10.6 %all-reduce.18 = (f32[4096]{0:T(1024)S(1)}, f32[8]{0:T(128)S(1)}, f32[9]{0:T(128)S(1)}) all-reduce(f32[4096]{0:T(1024)S(1)} %broadcast_select_fusion.19, f32[8]{0:T(128)S(1)} %convolution_bitcast_fusion.36, f32[9]{0:T(128)S(1)} %convolution_bitcast_fusion.35), channel_id=1, replica_groups=mesh['row'=4,'col'=8] {'row'}, use_global_device_ids=true, to_apply=%region_6.7 | all-reduce | flops 4113 | bytes 32904 | tf_op jit(solution)/shard_map/psum | solution.py:11
  154.1 30.7 %fusion.122 = f32[1,4096]{1,0:T(1,128)S(1)} fusion(f32[2048,1]{0,1:T(1,128)S(1)} %bitcast.507, f32[4096,2048]{1,0:T(8,128)} %param.79), kind=kOutput, calls=%fused_computation.248 | convolution fusion | flops 100663296 | bytes 33579008 | tf_op jit(solution)/shard_map/dot_general | solution.py:55
  184.7 35.8 %psum.389 = f32[4096]{0:T(1024)S(1)} all-reduce(f32[4096]{0:T(1024)S(1)} %bitcast.450), channel_id=1, replica_groups=mesh['row'=4,'col'=8] {'col'}, use_global_device_ids=true, to_apply=%region_7.8 | all-reduce | flops 4096 | bytes 32768 | tf_op jit(solution)/shard_map/psum | solution.py:55
  232.0 6.4 all-reduce.17
  241.9 10.3 %all-reduce.16 = (f32[4096]{0:T(1024)S(1)}, f32[8]{0:T(128)S(1)}, f32[9]{0:T(128)S(1)}) all-reduce(f32[4096]{0:T(1024)S(1)} %broadcast_select_fusion.17, f32[8]{0:T(128)S(1)} %convolution_bitcast_fusion.33, f32[9]{0:T(128)S(1)} %convolution_bitcast_fusion.32), channel_id=1, replica_groups=mesh['row'=4,'col'=8] {'row'}, use_global_device_ids=true, to_apply=%region_16.17 | all-reduce | flops 4113 | bytes 32904 | tf_op jit(solution)/shard_map/psum | solution.py:11
  253.3 30.7 %fusion.123 = f32[1,4096]{1,0:T(1,128)S(1)} fusion(f32[2048,1]{0,1:T(1,128)S(1)} %bitcast.508, f32[4096,2048]{1,0:T(8,128)} %param.79), kind=kOutput, calls=%fused_computation.249 | convolution fusion | flops 100663296 | bytes 33579008 | tf_op jit(solution)/shard_map/dot_general | solution.py:55
  284.0 33.0 %psum.396 = f32[4096]{0:T(1024)S(1)} all-reduce(f32[4096]{0:T(1024)S(1)} %bitcast.451), channel_id=1, replica_groups=mesh['row'=4,'col'=8] {'col'}, use_global_device_ids=true, to_apply=%region_17.18 | all-reduce | flops 4096 | bytes 32768 | tf_op jit(solution)/shard_map/psum | solution.py:55
  326.6 7.3 all-reduce.15
  337.3 10.6 %all-reduce.14 = (f32[4096]{0:T(1024)S(1)}, f32[8]{0:T(128)S(1)}, f32[9,1]{0,1:T(1,128)S(1)}) all-reduce(f32[4096]{0:T(1024)S(1)} %get-tuple-element.558, f32[8]{0:T(128)S(1)} %convolution_bitcast_fusion.30, f32[9,1]{0,1:T(1,128)S(1)} %convolution_bitcast_fusion.29), channel_id=1, replica_groups=mesh['row'=4,'col'=8] {'row'}, use_global_device_ids=true, to_apply=%region_26.27 | all-reduce | flops 4113 | bytes 32904 | tf_op jit(solution)/shard_map/psum | solution.py:11
  350.0 30.7 %fusion.125 = f32[1,4096]{1,0:T(1,128)S(1)} fusion(f32[2048,1]{0,1:T(1,128)S(1)} %bitcast.509, f32[4096,2048]{1,0:T(8,128)} %param.79), kind=kOutput, calls=%fused_computation.251 | convolution fusion | flops 100663296 | bytes 33579008 | tf_op jit(solution)/shard_map/dot_general | solution.py:55
  380.7 33.0 %psum.403 = f32[4096]{0:T(1024)S(1)} all-reduce(f32[4096]{0:T(1024)S(1)} %bitcast.452), channel_id=1, replica_groups=mesh['row'=4,'col'=8] {'col'}, use_global_device_ids=true, to_apply=%region_27.28 | all-reduce | flops 4096 | bytes 32768 | tf_op jit(solution)/shard_map/psum | solution.py:55
  423.1 6.4 all-reduce.13
  432.9 10.3 %all-reduce.12 = (f32[4096]{0:T(1024)S(1)}, f32[8]{0:T(128)S(1)}, f32[9,1]{0,1:T(1,128)S(1)}) all-reduce(f32[4096]{0:T(1024)S(1)} %get-tuple-element.555, f32[8]{0:T(128)S(1)} %convolution_bitcast_fusion.27, f32[9,1]{0,1:T(1,128)S(1)} %convolution_bitcast_fusion.26), channel_id=1, replica_groups=mesh['row'=4,'col'=8] {'row'}, use_global_device_ids=true, to_apply=%region_36.37 | all-reduce | flops 4113 | bytes 32904 | tf_op jit(solution)/shard_map/psum | solution.py:11
  444.8 30.7 %fusion.127 = f32[1,4096]{1,0:T(1,128)S(1)} fusion(f32[2048,1]{0,1:T(1,128)S(1)} %bitcast.510, f32[4096,2048]{1,0:T(8,128)} %param.79), kind=kOutput, calls=%fused_computation.253 | convolution fusion | flops 100663296 | bytes 33579008 | tf_op jit(solution)/shard_map/dot_general | solution.py:55
  475.5 33.0 %psum.410 = f32[4096]{0:T(1024)S(1)} all-reduce(f32[4096]{0:T(1024)S(1)} %bitcast.453), channel_id=1, replica_groups=mesh['row'=4,'col'=8] {'col'}, use_global_device_ids=true, to_apply=%region_37.38 | all-reduce | flops 4096 | bytes 32768 | tf_op jit(solution)/shard_map/psum | solution.py:55
  517.8 7.3 all-reduce.11
  528.5 10.6 %all-reduce.10 = (f32[4096]{0:T(1024)S(1)}, f32[8]{0:T(128)S(1)}, f32[9,1]{0,1:T(1,128)S(1)}) all-reduce(f32[4096]{0:T(1024)S(1)} %get-tuple-element.552, f32[8]{0:T(128)S(1)} %convolution_bitcast_fusion.24, f32[9,1]{0,1:T(1,128)S(1)} %convolution_bitcast_fusion.23), channel_id=1, replica_groups=mesh['row'=4,'col'=8] {'row'}, use_global_device_ids=true, to_apply=%region_46.47 | all-reduce | flops 4113 | bytes 32904 | tf_op jit(solution)/shard_map/psum | solution.py:11
  541.0 30.7 %fusion.129 = f32[1,4096]{1,0:T(1,128)S(1)} fusion(f32[2048,1]{0,1:T(1,128)S(1)} %bitcast.511, f32[4096,2048]{1,0:T(8,128)} %param.79), kind=kOutput, calls=%fused_computation.255 | convolution fusion | flops 100663296 | bytes 33579008 | tf_op jit(solution)/shard_map/dot_general | solution.py:55
  571.7 33.0 %psum.417 = f32[4096]{0:T(1024)S(1)} all-reduce(f32[4096]{0:T(1024)S(1)} %bitcast.454), channel_id=1, replica_groups=mesh['row'=4,'col'=8] {'col'}, use_global_device_ids=true, to_apply=%region_47.48 | all-reduce | flops 4096 | bytes 32768 | tf_op jit(solution)/shard_map/psum | solution.py:55
  624.0 10.3 %all-reduce.8 = (f32[4096]{0:T(1024)S(1)}, f32[8]{0:T(128)S(1)}, f32[9,1]{0,1:T(1,128)S(1)}) all-reduce(f32[4096]{0:T(1024)S(1)} %get-tuple-element.549, f32[8]{0:T(128)S(1)} %convolution_bitcast_fusion.21, f32[9,1]{0,1:T(1,128)S(1)} %convolution_bitcast_fusion.20), channel_id=1, replica_groups=mesh['row'=4,'col'=8] {'row'}, use_global_device_ids=true, to_apply=%region_56.57 | all-reduce | flops 4113 | bytes 32904 | tf_op jit(solution)/shard_map/psum | solution.py:11
  635.9 30.7 %fusion.131 = f32[1,4096]{1,0:T(1,128)S(1)} fusion(f32[2048,1]{0,1:T(1,128)S(1)} %bitcast.512, f32[4096,2048]{1,0:T(8,128)} %param.79), kind=kOutput, calls=%fused_computation.257 | convolution fusion | flops 100663296 | bytes 33579008 | tf_op jit(solution)/shard_map/dot_general | solution.py:55
  666.6 33.0 %psum.424 = f32[4096]{0:T(1024)S(1)} all-reduce(f32[4096]{0:T(1024)S(1)} %bitcast.455), channel_id=1, replica_groups=mesh['row'=4,'col'=8] {'col'}, use_global_device_ids=true, to_apply=%region_57.58 | all-reduce | flops 4096 | bytes 32768 | tf_op jit(solution)/shard_map/psum | solution.py:55
  708.8 7.3 all-reduce.7
  719.4 10.6 %all-reduce.6 = (f32[4096]{0:T(1024)S(1)}, f32[8]{0:T(128)S(1)}, f32[9,1]{0,1:T(1,128)S(1)}) all-reduce(f32[4096]{0:T(1024)S(1)} %get-tuple-element.546, f32[8]{0:T(128)S(1)} %convolution_bitcast_fusion.18, f32[9,1]{0,1:T(1,128)S(1)} %convolution_bitcast_fusion.17), channel_id=1, replica_groups=mesh['row'=4,'col'=8] {'row'}, use_global_device_ids=true, to_apply=%region_66.67 | all-reduce | flops 4113 | bytes 32904 | tf_op jit(solution)/shard_map/psum | solution.py:11
  732.0 30.7 %fusion.133 = f32[1,4096]{1,0:T(1,128)S(1)} fusion(f32[2048,1]{0,1:T(1,128)S(1)} %bitcast.513, f32[4096,2048]{1,0:T(8,128)} %param.79), kind=kOutput, calls=%fused_computation.259 | convolution fusion | flops 100663296 | bytes 33579008 | tf_op jit(solution)/shard_map/dot_general | solution.py:55
  762.7 33.0 %psum.431 = f32[4096]{0:T(1024)S(1)} all-reduce(f32[4096]{0:T(1024)S(1)} %bitcast.456), channel_id=1, replica_groups=mesh['row'=4,'col'=8] {'col'}, use_global_device_ids=true, to_apply=%region_67.68 | all-reduce | flops 4096 | bytes 32768 | tf_op jit(solution)/shard_map/psum | solution.py:55
  813.8 10.3 %all-reduce.4 = (f32[4096]{0:T(1024)S(1)}, f32[8]{0:T(128)S(1)}) all-reduce(f32[4096]{0:T(1024)S(1)} %get-tuple-element.543, f32[8]{0:T(128)S(1)} %convolution_bitcast_fusion.15), channel_id=1, replica_groups=mesh['row'=4,'col'=8] {'row'}, use_global_device_ids=true, to_apply=%region_75.76 | all-reduce | flops 4104 | bytes 32832 | tf_op jit(solution)/shard_map/psum | solution.py:11
  825.9 30.7 %fusion.135 = f32[1,4096]{1,0:T(1,128)S(1)} fusion(f32[2048,1]{0,1:T(1,128)S(1)} %bitcast.506, f32[4096,2048]{1,0:T(8,128)} %param.79), kind=kOutput, calls=%fused_computation.261 | convolution fusion | flops 100663296 | bytes 33579008 | tf_op jit(solution)/shard_map/dot_general | solution.py:55
  856.6 33.0 %psum.438 = f32[4096]{0:T(1024)S(1)} all-reduce(f32[4096]{0:T(1024)S(1)} %bitcast.457), channel_id=1, replica_groups=mesh['row'=4,'col'=8] {'col'}, use_global_device_ids=true, to_apply=%region_76.77 | all-reduce | flops 4096 | bytes 32768 | tf_op jit(solution)/shard_map/psum | solution.py:55
  (192 shorter events, 112.8 us)
Async XLA Ops:
  7.2 109.5 %all-reduce.22.cloned.1.call-start = ((), (), s32[]{:S(2)}) async-start(), calls=%async_computation | async-start | bytes 4194304 | tf_op jit(solution)/shard_map/psum | solution.py:11
  824.9 65.9 %copy-start = (f32[4096,8]{0,1:T(8,128)}, f32[4096,8]{0,1:T(8,128)S(1)}, u32[]{:S(2)}) copy-start(f32[4096,8]{0,1:T(8,128)S(1)} %scatter.189) | copy-start | bytes 393220
  890.0 0.9 copy-start.1
Sparse Core Ops, SparseCore 0:
  11.6 105.0 all-reduce.21
where the time goes:
time: 907 us; the launch traced here: 898 us
  blocking collectives  444 us (49%)
  matrix products  265 us (29%)
  waiting for transfers between devices  101 us (11%)
  between operations  31.3 us (3%)
  local copies, waits for them, and re-layouts  28.4 us (3%)
  other arithmetic  27.4 us (3%)
    psum x8, blocking collectives, shards(): image = lax.psum(jnp.dot(matrix, piece, precision=exact), 'col')  267 us
    dot_general x8, matrix products, shards(): image = lax.psum(jnp.dot(matrix, piece, precision=exact), 'col')  246 us
    psum x1, waiting for transfers between devices, spread(): return lax.psum(jnp.where(mine, value, jnp.zeros_like(value)), axis)  101 us
    psum x8, blocking collectives, spread(): return lax.psum(jnp.where(mine, value, jnp.zeros_like(value)), axis)  83.5 us
    psum x8, blocking collectives, shards(): lax.psum((jnp.sum(below * below), jnp.sum(jnp.where(row_ids == column + 1...  54.1 us
    psum x7, blocking collectives, shards(): inner = lax.psum(jnp.dot(current, refl, precision=exact), 'row')  40.1 us
  transfers between devices with their start and end apart: 1, of which 1 were waited for; matrix products, arithmetic and copies ran while one was open for 1% of the time, Pallas kernels for 0%

commit v1 on v0

--- a/solution.py
+++ b/solution.py
@@ -4,6 +4,11 @@
 from jax.sharding import PartitionSpec as P
 
 NB = 8
+
+
+def add_all(shard, axis):
+    parts = lax.all_gather(shard, axis)
+    return jnp.sum(parts, axis=0)
 
 
 def spread(value, axis, root):
@@ -52,7 +57,7 @@
             (jnp.dot(vector, refl, precision=exact), jnp.dot(picker, vector, precision=exact)),
             "row",
         )
-        image = lax.psum(jnp.dot(matrix, piece, precision=exact), "col")
+        image = add_all(jnp.dot(matrix, piece, precision=exact), "col")
         new_y = image - jnp.dot(wy_prod, coupling, precision=exact)
         new_t = -jnp.dot(factor, coupling, precision=exact)
         factor = factor.at[:, column].set(new_t).at[column, column].set(jnp.float32(1.0))

time: 907 us -> 886 us (0.977)
  blocking collectives: 444 us -> 422 us
    psum x8 -> x0, blocking collectives: 267 us -> none  [shards(): image = lax.psum(jnp.dot(matrix, piece, precision=exact), 'col')]
    all_gather x0 -> x8, blocking collectives: none -> 244 us  [add_all(): parts = lax.all_gather(shard, axis)]
where the time goes in v1:
time: 886 us; the launch traced here: 876 us
  blocking collectives  422 us (48%)
  matrix products  265 us (30%)
  waiting for transfers between devices  101 us (11%)
  between operations  31.4 us (4%)
  local copies, waits for them, and re-layouts  28.7 us (3%)
  other arithmetic  27.7 us (3%)
    dot_general x8, matrix products, shards(): image = add_all(jnp.dot(matrix, piece, precision=exact), 'col')  246 us
    all_gather x8, blocking collectives, add_all(): parts = lax.all_gather(shard, axis)  244 us
    psum x1, waiting for transfers between devices, spread(): return lax.psum(jnp.where(mine, value, jnp.zeros_like(value)), axis)  101 us
    psum x8, blocking collectives, spread(): return lax.psum(jnp.where(mine, value, jnp.zeros_like(value)), axis)  82.4 us
    psum x8, blocking collectives, shards(): lax.psum((jnp.sum(below * below), jnp.sum(jnp.where(row_ids == column + 1...  55.6 us
    psum x7, blocking collectives, shards(): inner = lax.psum(jnp.dot(current, refl, precision=exact), 'row')  39.5 us
    another operation x28, other arithmetic  18 us
  transfers between devices with their start and end apart: 1, of which 1 were waited for; matrix products, arithmetic and copies ran while one was open for 1% of the time, Pallas kernels for 0%

profile of v1, /device:TPU:0, one launch (start us, length us, event | category | flops | bytes accessed | tf_op | source)
XLA Modules:
  0.0 876.1 jit_solution(10953989410383108822)
XLA Ops:
  15.5 101.1 %all-reduce.22.cloned.1.call-done = f32[4096,8]{1,0:T(8,128)} async-done(((f32[4096,8]{1,0:T(8,128)}), f32[4096,8]{1,0:T(8,128)}) %all-reduce.22.cloned.1.call-update) | async-done | bytes 131088 | tf_op jit(solution)/shard_map/psum | solution.py:16
  116.7 15.4 %slice_reduce_fusion = (f32[4096]{0:T(1024)S(1)}, f32[4096]{0:T(1024)S(1)}, f32[4096]{0:T(1024)S(1)}, f32[4096]{0:T(1024)S(1)}, f32[4096]{0:T(1024)S(1)}, /*inde...) fusion(f32[4096,8]{1,0:T(8,128)} %all-reduce.22.cloned.1.call-done), kind=kLoop, calls=%fused_computation | loop fusion | bytes 262144 | tf_op jit(solution)/shard_map/slice | solution.py:33
  143.5 10.6 %all-reduce.18 = (f32[4096]{0:T(1024)S(1)}, f32[8]{0:T(128)S(1)}, f32[9]{0:T(128)S(1)}) all-reduce(f32[4096]{0:T(1024)S(1)} %broadcast_select_fusion.19, f32[8]{0:T(128)S(1)} %convolution_bitcast_fusion.36, f32[9]{0:T(128)S(1)} %convolution_bitcast_fusion.35), channel_id=1, replica_groups=mesh['row'=4,'col'=8] {'row'}, use_global_device_ids=true, to_apply=%region_6.7 | all-reduce | flops 4113 | bytes 32904 | tf_op jit(solution)/shard_map/psum | solution.py:16
  154.1 30.7 %fusion.122 = f32[1,4096]{1,0:T(1,128)S(1)} fusion(f32[2048,1]{0,1:T(1,128)S(1)} %bitcast.507, f32[4096,2048]{1,0:T(8,128)} %param.79), kind=kOutput, calls=%fused_computation.248 | convolution fusion | flops 100663296 | bytes 33579008 | tf_op jit(solution)/shard_map/dot_general | solution.py:60
  184.7 30.5 %all-gather = f32[32768]{0:T(1024)S(1)} all-gather(f32[4096]{0:T(1024)S(1)} %bitcast.450), channel_id=2, replica_groups=mesh['row'=4,'col'=8] {'col'}, dimensions={0}, use_global_device_ids=true | all-gather | bytes 147456 | tf_op jit(solution)/shard_map/all_gather | solution.py:10
  237.0 10.3 %all-reduce.16 = (f32[4096]{0:T(1024)S(1)}, f32[8]{0:T(128)S(1)}, f32[9]{0:T(128)S(1)}) all-reduce(f32[4096]{0:T(1024)S(1)} %broadcast_select_fusion.17, f32[8]{0:T(128)S(1)} %convolution_bitcast_fusion.33, f32[9]{0:T(128)S(1)} %convolution_bitcast_fusion.32), channel_id=1, replica_groups=mesh['row'=4,'col'=8] {'row'}, use_global_device_ids=true, to_apply=%region_16.17 | all-reduce | flops 4113 | bytes 32904 | tf_op jit(solution)/shard_map/psum | solution.py:16
  248.4 30.7 %fusion.123 = f32[1,4096]{1,0:T(1,128)S(1)} fusion(f32[2048,1]{0,1:T(1,128)S(1)} %bitcast.508, f32[4096,2048]{1,0:T(8,128)} %param.79), kind=kOutput, calls=%fused_computation.249 | convolution fusion | flops 100663296 | bytes 33579008 | tf_op jit(solution)/shard_map/dot_general | solution.py:60
  279.1 30.5 %all-gather.1 = f32[32768]{0:T(1024)S(1)} all-gather(f32[4096]{0:T(1024)S(1)} %bitcast.451), channel_id=3, replica_groups=mesh['row'=4,'col'=8] {'col'}, dimensions={0}, use_global_device_ids=true | all-gather | bytes 147456 | tf_op jit(solution)/shard_map/all_gather | solution.py:10
  319.5 7.1 all-reduce.15
  329.9 10.3 %all-reduce.14 = (f32[4096]{0:T(1024)S(1)}, f32[8]{0:T(128)S(1)}, f32[9,1]{0,1:T(1,128)S(1)}) all-reduce(f32[4096]{0:T(1024)S(1)} %get-tuple-element.566, f32[8]{0:T(128)S(1)} %convolution_bitcast_fusion.30, f32[9,1]{0,1:T(1,128)S(1)} %convolution_bitcast_fusion.29), channel_id=1, replica_groups=mesh['row'=4,'col'=8] {'row'}, use_global_device_ids=true, to_apply=%region_26.27 | all-reduce | flops 4113 | bytes 32904 | tf_op jit(solution)/shard_map/psum | solution.py:16
  342.2 30.7 %fusion.125 = f32[1,4096]{1,0:T(1,128)S(1)} fusion(f32[2048,1]{0,1:T(1,128)S(1)} %bitcast.509, f32[4096,2048]{1,0:T(8,128)} %param.79), kind=kOutput, calls=%fused_computation.251 | convolution fusion | flops 100663296 | bytes 33579008 | tf_op jit(solution)/shard_map/dot_general | solution.py:60
  372.9 30.5 %all-gather.2 = f32[32768]{0:T(1024)S(1)} all-gather(f32[4096]{0:T(1024)S(1)} %bitcast.452), channel_id=4, replica_groups=mesh['row'=4,'col'=8] {'col'}, dimensions={0}, use_global_device_ids=true | all-gather | bytes 147456 | tf_op jit(solution)/shard_map/all_gather | solution.py:10
  412.8 6.9 all-reduce.13
  423.2 10.3 %all-reduce.12 = (f32[4096]{0:T(1024)S(1)}, f32[8]{0:T(128)S(1)}, f32[9,1]{0,1:T(1,128)S(1)}) all-reduce(f32[4096]{0:T(1024)S(1)} %get-tuple-element.563, f32[8]{0:T(128)S(1)} %convolution_bitcast_fusion.27, f32[9,1]{0,1:T(1,128)S(1)} %convolution_bitcast_fusion.26), channel_id=1, replica_groups=mesh['row'=4,'col'=8] {'row'}, use_global_device_ids=true, to_apply=%region_36.37 | all-reduce | flops 4113 | bytes 32904 | tf_op jit(solution)/shard_map/psum | solution.py:16
  435.1 30.7 %fusion.127 = f32[1,4096]{1,0:T(1,128)S(1)} fusion(f32[2048,1]{0,1:T(1,128)S(1)} %bitcast.510, f32[4096,2048]{1,0:T(8,128)} %param.79), kind=kOutput, calls=%fused_computation.253 | convolution fusion | flops 100663296 | bytes 33579008 | tf_op jit(solution)/shard_map/dot_general | solution.py:60
  465.8 30.7 %all-gather.3 = f32[32768]{0:T(1024)S(1)} all-gather(f32[4096]{0:T(1024)S(1)} %bitcast.453), channel_id=5, replica_groups=mesh['row'=4,'col'=8] {'col'}, dimensions={0}, use_global_device_ids=true | all-gather | bytes 147456 | tf_op jit(solution)/shard_map/all_gather | solution.py:10
  505.9 7.0 all-reduce.11
  516.3 10.3 %all-reduce.10 = (f32[4096]{0:T(1024)S(1)}, f32[8]{0:T(128)S(1)}, f32[9,1]{0,1:T(1,128)S(1)}) all-reduce(f32[4096]{0:T(1024)S(1)} %get-tuple-element.560, f32[8]{0:T(128)S(1)} %convolution_bitcast_fusion.24, f32[9,1]{0,1:T(1,128)S(1)} %convolution_bitcast_fusion.23), channel_id=1, replica_groups=mesh['row'=4,'col'=8] {'row'}, use_global_device_ids=true, to_apply=%region_46.47 | all-reduce | flops 4113 | bytes 32904 | tf_op jit(solution)/shard_map/psum | solution.py:16
  528.3 30.7 %fusion.129 = f32[1,4096]{1,0:T(1,128)S(1)} fusion(f32[2048,1]{0,1:T(1,128)S(1)} %bitcast.511, f32[4096,2048]{1,0:T(8,128)} %param.79), kind=kOutput, calls=%fused_computation.255 | convolution fusion | flops 100663296 | bytes 33579008 | tf_op jit(solution)/shard_map/dot_general | solution.py:60
  559.0 30.6 %all-gather.4 = f32[32768]{0:T(1024)S(1)} all-gather(f32[4096]{0:T(1024)S(1)} %bitcast.454), channel_id=6, replica_groups=mesh['row'=4,'col'=8] {'col'}, dimensions={0}, use_global_device_ids=true | all-gather | bytes 147456 | tf_op jit(solution)/shard_map/all_gather | solution.py:10
  599.2 7.0 all-reduce.9
  609.5 10.3 %all-reduce.8 = (f32[4096]{0:T(1024)S(1)}, f32[8]{0:T(128)S(1)}, f32[9,1]{0,1:T(1,128)S(1)}) all-reduce(f32[4096]{0:T(1024)S(1)} %get-tuple-element.557, f32[8]{0:T(128)S(1)} %convolution_bitcast_fusion.21, f32[9,1]{0,1:T(1,128)S(1)} %convolution_bitcast_fusion.20), channel_id=1, replica_groups=mesh['row'=4,'col'=8] {'row'}, use_global_device_ids=true, to_apply=%region_56.57 | all-reduce | flops 4113 | bytes 32904 | tf_op jit(solution)/shard_map/psum | solution.py:16
  621.4 30.7 %fusion.131 = f32[1,4096]{1,0:T(1,128)S(1)} fusion(f32[2048,1]{0,1:T(1,128)S(1)} %bitcast.512, f32[4096,2048]{1,0:T(8,128)} %param.79), kind=kOutput, calls=%fused_computation.257 | convolution fusion | flops 100663296 | bytes 33579008 | tf_op jit(solution)/shard_map/dot_general | solution.py:60
  652.1 30.5 %all-gather.5 = f32[32768]{0:T(1024)S(1)} all-gather(f32[4096]{0:T(1024)S(1)} %bitcast.455), channel_id=7, replica_groups=mesh['row'=4,'col'=8] {'col'}, dimensions={0}, use_global_device_ids=true | all-gather | bytes 147456 | tf_op jit(solution)/shard_map/all_gather | solution.py:10
  691.9 7.0 all-reduce.7
  702.3 10.3 %all-reduce.6 = (f32[4096]{0:T(1024)S(1)}, f32[8]{0:T(128)S(1)}, f32[9,1]{0,1:T(1,128)S(1)}) all-reduce(f32[4096]{0:T(1024)S(1)} %get-tuple-element.554, f32[8]{0:T(128)S(1)} %convolution_bitcast_fusion.18, f32[9,1]{0,1:T(1,128)S(1)} %convolution_bitcast_fusion.17), channel_id=1, replica_groups=mesh['row'=4,'col'=8] {'row'}, use_global_device_ids=true, to_apply=%region_66.67 | all-reduce | flops 4113 | bytes 32904 | tf_op jit(solution)/shard_map/psum | solution.py:16
  714.5 30.7 %fusion.133 = f32[1,4096]{1,0:T(1,128)S(1)} fusion(f32[2048,1]{0,1:T(1,128)S(1)} %bitcast.513, f32[4096,2048]{1,0:T(8,128)} %param.79), kind=kOutput, calls=%fused_computation.259 | convolution fusion | flops 100663296 | bytes 33579008 | tf_op jit(solution)/shard_map/dot_general | solution.py:60
  745.2 30.5 %all-gather.6 = f32[32768]{0:T(1024)S(1)} all-gather(f32[4096]{0:T(1024)S(1)} %bitcast.456), channel_id=8, replica_groups=mesh['row'=4,'col'=8] {'col'}, dimensions={0}, use_global_device_ids=true | all-gather | bytes 147456 | tf_op jit(solution)/shard_map/all_gather | solution.py:10
  785.0 7.0 all-reduce.5
  794.4 10.3 %all-reduce.4 = (f32[4096]{0:T(1024)S(1)}, f32[8]{0:T(128)S(1)}) all-reduce(f32[4096]{0:T(1024)S(1)} %get-tuple-element.551, f32[8]{0:T(128)S(1)} %convolution_bitcast_fusion.15), channel_id=1, replica_groups=mesh['row'=4,'col'=8] {'row'}, use_global_device_ids=true, to_apply=%region_75.76 | all-reduce | flops 4104 | bytes 32832 | tf_op jit(solution)/shard_map/psum | solution.py:16
  806.5 30.7 %fusion.135 = f32[1,4096]{1,0:T(1,128)S(1)} fusion(f32[2048,1]{0,1:T(1,128)S(1)} %bitcast.506, f32[4096,2048]{1,0:T(8,128)} %param.79), kind=kOutput, calls=%fused_computation.261 | convolution fusion | flops 100663296 | bytes 33579008 | tf_op jit(solution)/shard_map/dot_general | solution.py:60
  837.2 30.6 %all-gather.7 = f32[32768]{0:T(1024)S(1)} all-gather(f32[4096]{0:T(1024)S(1)} %bitcast.457), channel_id=9, replica_groups=mesh['row'=4,'col'=8] {'col'}, dimensions={0}, use_global_device_ids=true | all-gather | bytes 147456 | tf_op jit(solution)/shard_map/all_gather | solution.py:10
  (208 shorter events, 113.8 us)
Async XLA Ops:
  7.2 109.5 %all-reduce.22.cloned.1.call-start = ((), (), s32[]{:S(2)}) async-start(), calls=%async_computation | async-start | bytes 4194304 | tf_op jit(solution)/shard_map/psum | solution.py:16
  805.4 63.7 %copy-start = (f32[4096,8]{0,1:T(8,128)}, f32[4096,8]{0,1:T(8,128)S(1)}, u32[]{:S(2)}) copy-start(f32[4096,8]{0,1:T(8,128)S(1)} %scatter.189) | copy-start | bytes 393220
  868.2 0.9 copy-start.1
Sparse Core Ops, SparseCore 0:
  11.6 105.0 all-reduce.21
